TPU v7x, 128 devices: a whole 4x4x4 slice. The times are simulated.
128 devices in a mesh: gx: 4 (over y_lo, core), gy: 8 (over x, y_hi), gz: 4 (over z).
Axes of the slice: x: 4, y: 4 (y_hi: 2, y_lo: 2; y = y_hi * 2 + y_lo), z: 4, core: 2. Of those that a mesh axis runs over, the one named last changes fastest.
Arguments:
- positions: float32 [3, 4, 8, 4, 4096], P(None, 'gx', 'gy', 'gz'), may hold values from 0 to 4, as said below
- velocities: float32 [3, 4, 8, 4, 4096], P(None, 'gx', 'gy', 'gz'), may hold values from -6 to 6
- strength: float32 [4, 8, 4, 4096], P('gx', 'gy', 'gz'), may hold values from 0.5 to 2
- charge: float32 [4, 8, 4, 4096], P('gx', 'gy', 'gz'), may hold values from -5 to 5
- bond_stiffness: float32 [2, 4, 8, 4, 4096], P(None, 'gx', 'gy', 'gz'), may hold values from 0.5 to 4
- bond_partner: int32 [2, 4, 8, 4, 4096], P(None, 'gx', 'gy', 'gz'), may hold values from 0 to 18431, as said below
- pair_blocks: int32 [4, 8, 4, 32, 8], P('gx', 'gy', 'gz'), may hold values from 0 to 143, as said below
- tile_count: int32 [4, 8, 4], P('gx', 'gy', 'gz'), may hold values from 1024 to 4096, as said below
- block_cell: int32 [4, 8, 4, 32], P('gx', 'gy', 'gz'), may hold values from 0 to 1023
- cell_frac: float32 [3, 1024], replicated, may hold values from 0 to 1
- bond_force: float32 [3, 4, 8, 4, 4096], P(None, 'gx', 'gy', 'gz'), may hold values from -6 to 6
- pair_force: float32 [3, 4, 8, 4, 4096], P(None, 'gx', 'gy', 'gz'), may hold values from -6 to 6
- far_force: float32 [3, 4, 8, 4, 4096], P(None, 'gx', 'gy', 'gz'), may hold values from -6 to 6
Outputs:
- positions_out: float32 [3, 4, 8, 4, 4096], P(None, 'gx', 'gy', 'gz')
- velocities_out: float32 [3, 4, 8, 4, 4096], P(None, 'gx', 'gy', 'gz')
Inputs may be any that keep to these rules, and one draw needn't show every extreme that they name: `positions`: each bead lies inside the unit cube of its block. `tile_count`: live beads of a tile fill its slots from 0 upward; some tile is full in every draw. `bond_partner`: A live bead's partners are live beads of its own block or of one of the six blocks sharing a face with it; an empty slot names its own column. `pair_blocks`: each row begins with the block itself and then lists distinct blocks that share a face, an edge or a corner with it.
All inputs are finite; a program needn't handle non-finite values.
Results may differ from a plain program's by a relative error of at most 0.0003.
Values sent between devices are 32-bit elements; how exact they have to be, the bound alone decides.
A program may use at most 64 MiB of HBM per device.

v0:
```python
import math

import jax
import jax.numpy as jnp
from jax import lax
from jax.experimental import pallas as pl
from jax.experimental.pallas import tpu as pltpu
from jax.sharding import PartitionSpec as P

MESH = pl.DeviceIdType.MESH
SBX, SBY, SBZ = 4, 4, 2
BLK = 128
NB = SBX * SBY * SBZ
EX, EY, EZ = SBX + 2, SBY + 2, SBZ + 2
NE = EX * EY * EZ
CELLS = 1024
AXES = ("gx", "gy", "gz")

inner_step = 0.1
gauss_width = 0.25
pair_scale = 0.1
soften = 1.0
coulomb = 0.02
half_step = 0.5 * inner_step
outer_half = 2.0 * inner_step

rate = 1.0 / (2.0 * gauss_width * gauss_width)
bits = rate / math.log(2.0)
pair_factor = pair_scale / (gauss_width * gauss_width) * math.exp(-rate) / (bits * bits)

FACES = ((-1, 0, 0), (1, 0, 0), (0, -1, 0), (0, 1, 0), (0, 0, -1), (0, 0, 1))
AROUND = tuple(
    (dx, dy, dz)
    for dx in (-1, 0, 1)
    for dy in (-1, 0, 1)
    for dz in (-1, 0, 1)
    if (dx, dy, dz) != (0, 0, 0)
)
FACE_SLOTS = tuple(AROUND.index(d) for d in FACES)
SIZES = (4, 8, 4)

F32 = jnp.float32
BF16 = jnp.bfloat16


def row_ids(n=4):
    return lax.broadcasted_iota(jnp.int32, (n, BLK), 0)


def rows4(a, b, c, d):
    r = row_ids()
    return jnp.where(r == 0, a, jnp.where(r == 1, b, jnp.where(r == 2, c, d)))


def place(b):
    return b // (SBY * SBZ) + 1, b // SBZ % SBY + 1, b % SBZ + 1


def lane_gather(values, lanes):
    numbers = lax.GatherDimensionNumbers(
        offset_dims=(),
        collapsed_slice_dims=(1,),
        start_index_map=(1,),
        operand_batching_dims=(0,),
        start_indices_batching_dims=(0,),
    )
    return lax.gather(
        values,
        lanes[..., None],
        numbers,
        slice_sizes=(1, 1),
        mode=lax.GatherScatterMode.PROMISE_IN_BOUNDS,
    )


def thirds(value):
    high = value.astype(BF16).astype(F32)
    rest = value - high
    middle = rest.astype(BF16).astype(F32)
    return high, middle, rest - middle


def send_box(step, inner, ghost):
    count = inner
    if step == 0:
        return pl.ds(1, count)
    if ghost:
        return pl.ds(0 if step > 0 else count + 1, 1)
    return pl.ds(count if step > 0 else 1, 1)


def box(direction, ghost):
    return tuple(
        send_box(s, inner, ghost) for s, inner in zip(direction, (SBX, SBY, SBZ))
    )


def kernel(
    pos,
    vel,
    stren,
    chg,
    stiff,
    part,
    bforce,
    pforce,
    fforce,
    frac,
    frac_s,
    pairs,
    cell,
    count,
    xo,
    vo,
    hood0,
    hood1,
    hood2,
    hood3,
    vbuf,
    qbuf,
    near,
    pull,
    left,
    centre,
    part0,
    part1,
    part2,
    got0,
    got1,
    got2,
    hs,
    hr,
    ms,
    mr,
):
    me = tuple(lax.axis_index(a) for a in AXES)

    def device(shift):
        return tuple(lax.rem(m + (s + n), n) for m, s, n in zip(me, shift, SIZES))

    barrier = pltpu.get_barrier_semaphore()
    peers = set(AROUND)
    for axis, n in ((2, 4), (0, 4), (1, 8)):
        for o in range(2, n - 1):
            peers.add(tuple(o if a == axis else 0 for a in range(3)))
    peers = sorted(peers)
    for shift in peers:
        pl.semaphore_signal(barrier, inc=1, device_id=device(shift), device_id_type=MESH)

    rows = row_ids()
    xyz = rows < 3
    lanes = lax.broadcasted_iota(jnp.int32, (1, BLK), 1)

    def halo(hood, which, slots):
        return [
            pltpu.make_async_remote_copy(
                src_ref=hood.at[box(AROUND[d], False)],
                dst_ref=hood.at[box(AROUND[d], True)],
                send_sem=hs.at[which, d],
                recv_sem=hr.at[which, d],
                device_id=device(AROUND[d]),
                device_id_type=MESH,
            )
            for d in slots
        ]

    def arrive(hood, copies, slots):
        for copy, d in zip(copies, slots):
            copy.wait_recv()
            dx, dy, dz = AROUND[d]
            shift = rows4(-SBX * dx * 1.0, -SBY * dy * 1.0, -SBZ * dz * 1.0, 0.0)
            ghost = box(AROUND[d], True)
            hood[ghost] = hood[ghost] + shift

    def begin(b, _):
        px, py, pz = place(b)
        live = jnp.where(b * BLK + lanes < count[0], 1.0, 0.0)
        qbuf[b] = chg[b] * live
        x = rows4(pos[0, b], pos[1, b], pos[2, b], stren[b] * live)
        v = [
            vel[d, b]
            + outer_half * fforce[d, b]
            + inner_step * pforce[d, b]
            + half_step * bforce[d, b]
            for d in range(3)
        ]
        v = rows4(v[0], v[1], v[2], 0.0)
        vbuf[b] = v
        hood0[px, py, pz] = x + inner_step * v
        return 0

    lax.fori_loop(0, NB, begin, 0, unroll=4)
    for d in range(3):
        for k in range(8):
            centre[d, k : k + 1, :] = frac[d : d + 1, k * BLK : (k + 1) * BLK] * (
                1.0 * SIZES[d] * (SBX, SBY, SBZ)[d]
            )

    pl.semaphore_wait(barrier, len(peers))
    copies0 = halo(hood0, 0, FACE_SLOTS)
    for copy in copies0:
        copy.start()

    def bond(hood, b, px, py, pz):
        own = hood[px, py, pz]
        home = (px * EY + py) * EZ + pz
        tiles = [own] + [hood[px + dx, py + dy, pz + dz] for dx, dy, dz in FACES]
        total = jnp.zeros((4, BLK), F32)
        for k in range(2):
            column = part[k, b]
            slot = jnp.broadcast_to(column & (BLK - 1), (4, BLK))
            away = jnp.broadcast_to((column >> 7) - home, (4, BLK))
            other = lane_gather(own, slot)
            for tile, (dx, dy, dz) in zip(tiles[1:], FACES):
                offset = (dx * EY + dy) * EZ + dz
                other = jnp.where(away == offset, lane_gather(tile, slot), other)
            total = total + stiff[k, b] * (other - own)
        return own, jnp.where(xyz, total, 0.0)

    def bond_step(hood, after):
        def body(b, _):
            px, py, pz = place(b)
            own, force = bond(hood, b, px, py, pz)
            v = vbuf[b] + inner_step * force
            vbuf[b] = v
            after[px, py, pz] = own + inner_step * v
            return 0

        lax.fori_loop(0, NB, body, 0, unroll=4)

    def bond_kick(hood, size):
        def body(b, _):
            px, py, pz = place(b)
            _, force = bond(hood, b, px, py, pz)
            vbuf[b] = vbuf[b] + size * force
            return 0

        lax.fori_loop(0, NB, body, 0, unroll=4)

    middle = rows4(0.5 * SBX, 0.5 * SBY, 0.5 * SBZ, 0.0)

    def square_sum(z):
        return jnp.sum(jnp.where(xyz, z * z, 0.0), axis=0, keepdims=True)

    def prepare(hood):
        ones = jnp.where(xyz, 1.0, 0.0)
        blank = jnp.zeros((4, BLK), F32)

        def body(e, _):
            tile = hood[e // (EY * EZ), e // EZ % EY, e % EZ]
            z = tile - middle
            high, mid, low = thirds(jnp.where(xyz, z, -bits * square_sum(z)))
            near[e] = jnp.concatenate(
                [high, mid, low, high, mid, high, ones, blank], axis=0
            ).astype(BF16)
            a = tile[3:4]
            high, mid, low = thirds(jnp.where(xyz, z * a, a))
            pull[e] = jnp.concatenate([high, mid, low, blank], axis=0).astype(BF16)
            return 0

        lax.fori_loop(0, NE, body, 0, unroll=4)

    def prepare_own(hood):
        def body(b, _):
            px, py, pz = place(b)
            z = hood[px, py, pz] - middle
            high, mid, low = thirds(jnp.where(xyz, (2.0 * bits) * z, 1.0))
            ph, pm, pw = thirds(bits - bits * square_sum(z))
            stack = jnp.concatenate(
                [
                    high,
                    high,
                    high,
                    mid,
                    mid,
                    low,
                    rows4(ph, pm, pw, 0.0),
                    jnp.zeros((4, BLK), F32),
                ],
                axis=0,
            )
            left[b] = stack.T.astype(BF16)
            return 0

        lax.fori_loop(0, NB, body, 0, unroll=4)

    def pair(hood, c):
        px, py, pz = place(c)
        mine = left[c]
        acc = jnp.zeros((BLK, 16), F32)
        for k in range(0, 8, 2):
            e0, e1 = pairs[c, k], pairs[c, k + 1]
            t = jnp.dot(
                mine,
                jnp.concatenate([near[e0], near[e1]], axis=1),
                preferred_element_type=F32,
            )
            r = jnp.maximum(t, 0.0)
            w = jnp.exp2(t) * (r * r)
            high = w.astype(BF16)
            low = (w - high.astype(F32)).astype(BF16)
            y = jnp.concatenate([pull[e0], pull[e1]], axis=1)
            over = (((1,), (1,)), ((), ()))
            acc = acc + lax.dot_general(high, y, over, preferred_element_type=F32)
            acc = acc + lax.dot_general(low, y, over, preferred_element_type=F32)
        s = acc.T
        f = s[0:4] + s[4:8] + s[8:12]
        tile = hood[px, py, pz]
        z = tile - middle
        force = (pair_factor * tile[3:4]) * (z * f[3:4] - f)
        return tile, jnp.where(xyz, force, 0.0)

    GROUP = 4

    def pair_step(hood, after):
        def body(g, _):
            for j in range(GROUP):
                c = g * GROUP + j
                px, py, pz = place(c)
                own, force = pair(hood, c)
                v = vbuf[c] + (2.0 * inner_step) * force
                vbuf[c] = v
                after[px, py, pz] = own + inner_step * v
            return 0

        lax.fori_loop(0, NB // GROUP, body, 0)

    def pair_kick(hood, lo, hi):
        def body(g, _):
            for j in range(GROUP):
                c = g * GROUP + j
                _, force = pair(hood, c)
                vbuf[c] = vbuf[c] + inner_step * force
            return 0

        lax.fori_loop(lo // GROUP, hi // GROUP, body, 0)

    arrive(hood0, copies0, FACE_SLOTS)
    bond_step(hood0, hood1)
    every = tuple(range(len(AROUND)))
    copies1 = halo(hood1, 1, every)
    for copy in copies1:
        copy.start()
    prepare_own(hood1)
    arrive(hood1, copies1, every)
    prepare(hood1)
    bond_kick(hood1, inner_step)
    pair_step(hood1, hood2)
    copies2 = halo(hood2, 2, FACE_SLOTS)
    for copy in copies2:
        copy.start()
    arrive(hood2, copies2, FACE_SLOTS)
    bond_step(hood2, hood3)
    copies3 = halo(hood3, 3, every)
    for copy in copies3:
        copy.start()

    cell_ids = lax.broadcasted_iota(jnp.int32, (8, BLK), 0) * BLK + lax.broadcasted_iota(
        jnp.int32, (8, BLK), 1
    )
    corner = rows4(
        (me[0] * SBX).astype(F32), (me[1] * SBY).astype(F32), (me[2] * SBZ).astype(F32), 0.0
    )

    def gather_moments(b, totals):
        px, py, pz = place(b)
        tile = hood3[px, py, pz]
        for d in range(3):
            xo[d, b] = tile[d : d + 1]
        sums = jnp.sum(
            qbuf[b] * jnp.where(xyz, tile + corner, 1.0), axis=1, keepdims=True
        )
        here = cell_ids == cell[b]
        return tuple(
            total + jnp.where(here, sums[d : d + 1], 0.0) for d, total in enumerate(totals)
        )

    zero = jnp.zeros((8, BLK), F32)
    moments = lax.fori_loop(0, NB, gather_moments, (zero, zero, zero, zero), unroll=4)
    for d in range(4):
        part0[d] = moments[d]

    stages = ((2, 4, part0, got0, 0), (0, 4, part1, got1, 3), (1, 8, part2, got2, 6))

    def spread(stage):
        axis, n, mine, got, base = stages[stage]
        return [
            pltpu.make_async_remote_copy(
                src_ref=mine,
                dst_ref=got.at[o - 1],
                send_sem=ms.at[base + o - 1],
                recv_sem=mr.at[base + o - 1],
                device_id=device(tuple(o if a == axis else 0 for a in range(3))),
                device_id_type=MESH,
            )
            for o in range(1, n)
        ]

    def collect(stage, copies):
        axis, n, mine, got, base = stages[stage]
        for copy in copies:
            copy.wait_recv()
        total = mine[...]
        for o in range(1, n):
            total = total + got[o - 1]
        return total

    spread0 = spread(0)
    for copy in spread0:
        copy.start()
    prepare_own(hood3)
    arrive(hood3, copies3, every)
    prepare(hood3)
    bond_kick(hood3, half_step)
    pair_kick(hood3, 0, 8)
    part1[...] = collect(0, spread0)
    spread1 = spread(1)
    for copy in spread1:
        copy.start()
    pair_kick(hood3, 8, 16)
    part2[...] = collect(1, spread1)
    spread2 = spread(2)
    for copy in spread2:
        copy.start()
    pair_kick(hood3, 16, 32)
    totals = collect(2, spread2)

    charge_sum = totals[3]
    places = [centre[d] for d in range(3)]
    dipole = [totals[d] - charge_sum * places[d] for d in range(3)]

    def finish(b, _):
        target = cell[b]
        away = [
            frac_s[d, target] * (1.0 * SIZES[d] * (SBX, SBY, SBZ)[d]) - places[d]
            for d in range(3)
        ]
        inverse = lax.rsqrt(
            away[0] * away[0] + away[1] * away[1] + away[2] * away[2] + soften * soften
        )
        cube = inverse * inverse * inverse
        fifth = cube * inverse * inverse
        along = dipole[0] * away[0] + dipole[1] * away[1] + dipole[2] * away[2]
        gain = charge_sum * cube + 3.0 * along * fifth
        field = [
            jnp.sum(gain * away[d] - dipole[d] * cube, axis=(0, 1), keepdims=True)
            for d in range(3)
        ]
        size = (outer_half * coulomb) * qbuf[b]
        v = vbuf[b]
        for d in range(3):
            vo[d, b] = v[d : d + 1] + size * field[d]
        return 0

    lax.fori_loop(0, NB, finish, 0, unroll=4)

    for copies in (copies0, copies1, copies2, copies3, spread0, spread1, spread2):
        for copy in copies:
            copy.wait_send()


def per_device(
    positions,
    velocities,
    strength,
    charge,
    bond_stiffness,
    bond_partner,
    pair_blocks,
    tile_count,
    block_cell,
    cell_frac,
    bond_force,
    pair_force,
    far_force,
):
    lines = lambda value, n: value.reshape(n, NB, 1, BLK)
    vmem = pl.BlockSpec(memory_space=pltpu.VMEM)
    smem = pl.BlockSpec(memory_space=pltpu.SMEM)
    hood = pltpu.VMEM((EX, EY, EZ, 4, BLK), F32)
    out = jax.ShapeDtypeStruct((3, NB, 1, BLK), F32)
    x, v = pl.pallas_call(
        kernel,
        out_shape=(out, out),
        in_specs=[vmem] * 10 + [smem] * 4,
        out_specs=(vmem, vmem),
        scratch_shapes=[
            hood,
            hood,
            hood,
            hood,
            pltpu.VMEM((NB, 4, BLK), F32),
            pltpu.VMEM((NB, 1, BLK), F32),
            pltpu.VMEM((NE, 32, BLK), BF16),
            pltpu.VMEM((NE, 16, BLK), BF16),
            pltpu.VMEM((NB, BLK, 32), BF16),
            pltpu.VMEM((3, 8, BLK), F32),
            pltpu.VMEM((4, 8, BLK), F32),
            pltpu.VMEM((4, 8, BLK), F32),
            pltpu.VMEM((4, 8, BLK), F32),
            pltpu.VMEM((3, 4, 8, BLK), F32),
            pltpu.VMEM((3, 4, 8, BLK), F32),
            pltpu.VMEM((7, 4, 8, BLK), F32),
            pltpu.SemaphoreType.DMA((4, 26)),
            pltpu.SemaphoreType.DMA((4, 26)),
            pltpu.SemaphoreType.DMA((13,)),
            pltpu.SemaphoreType.DMA((13,)),
        ],
        compiler_params=pltpu.CompilerParams(
            collective_id=0, has_side_effects=True, vmem_limit_bytes=48 * 1024 * 1024
        ),
        name="outer_step",
    )(
        lines(positions, 3),
        lines(velocities, 3),
        strength.reshape(NB, 1, BLK),
        charge.reshape(NB, 1, BLK),
        lines(bond_stiffness, 2),
        lines(bond_partner, 2),
        lines(bond_force, 3),
        lines(pair_force, 3),
        lines(far_force, 3),
        cell_frac,
        cell_frac,
        pair_blocks.reshape(NB, 8),
        block_cell.reshape(NB),
        tile_count.reshape(1),
    )
    return x.reshape(positions.shape), v.reshape(velocities.shape)


def solution(mesh):
    vector = P(None, "gx", "gy", "gz", None)
    scalar = P("gx", "gy", "gz", None)
    in_specs = (
        vector,
        vector,
        scalar,
        scalar,
        vector,
        vector,
        P("gx", "gy", "gz", None, None),
        P("gx", "gy", "gz"),
        scalar,
        P(),
        vector,
        vector,
        vector,
    )
    return jax.shard_map(
        per_device, mesh=mesh, in_specs=in_specs, out_specs=(vector, vector), check_vma=False
    )
```

profile of v0, /device:TPU:1, one launch (start us, length us, event | category | flops | bytes accessed | tf_op | source)
XLA Modules:
  0.0 82.2 jit_solution(13054962067776836287)
XLA Ops:
  1.3 0.0 copy-start.11
  1.3 0.0 copy-start.8
  1.3 0.0 copy-start
  1.3 0.7 copy-done.11
  2.0 0.1 copy.18
  2.0 0.0 copy-start.10
  2.0 0.0 copy-done.8
  2.0 0.0 copy-done
  2.0 0.6 copy-done.10
  2.7 0.0 copy-start.1
  2.7 0.8 copy-done.1
  3.5 0.0 copy-start.2
  3.5 0.8 copy-done.2
  4.3 0.0 copy-start.3
  4.3 0.8 copy-done.3
  5.1 0.0 copy-start.4
  5.1 0.8 copy-done.4
  5.9 0.0 copy-start.5
  5.9 0.8 copy-done.5
  6.7 0.0 copy-start.6
  6.7 0.8 copy-done.6
  7.5 0.0 copy-start.7
  7.5 0.8 copy-done.7
  8.2 0.0 copy-start.9
  8.2 0.7 copy-done.9
  8.9 72.0 %outer_step.1 = (f32[3,32,1,128]{3,2,1,0:T(1,128)S(1)}, f32[3,32,1,128]{3,2,1,0:T(1,128)S(1)}) custom-call(f32[3,32,1,128]{3,2,1,0:T(1,128)S(1)} %bitcast.20, f32[3,32,1,128]{3,2,1,0:T(1,128)S(1)} %bitcast.21, f32[32,1,128]{2,1,0:T(1,128)S(1)} %bitcast.29, f32[32,1,128]{2,1,0:T(1,128)S(1)} %bitcast.30, f32[2,32,1,128]{3,2,1,0:T(1,128)S(1)} %bitcast.27, ...), custom_call_target="tpu_custom_call" | custom-call | tf_op jit(solution)/shard_map/outer_step/pallas_call | solution.py:482
  81.0 0.6 copy.24
  81.6 0.6 copy.25
Async XLA Ops:
  1.3 0.7 copy-start.11
  1.3 0.8 copy-start.8
  1.3 0.8 copy-start
  2.0 0.7 copy-start.10
  2.7 0.8 copy-start.1
  3.5 0.8 copy-start.2
  4.3 0.8 copy-start.3
  5.1 0.8 copy-start.4
  5.9 0.8 copy-start.5
  6.7 0.8 copy-start.6
  7.5 0.8 copy-start.7
  8.2 0.7 copy-start.9
where the time goes:
time: 82.9 us; the launch traced here: 82.2 us
  Pallas kernels  72 us (87%)
  local copies, waits for them, and re-layouts  8.86 us (11%)
  between operations  1.32 us (2%)
    pallas_call x1, Pallas kernels, per_device(): pl.pallas_call(kernel, out_shape=(out, out), in_specs=[vmem] * 10 + [smem...  72 us
    unnamed x27, local copies, waits for them, and re-layouts  8.86 us

commit v1 on v0

v1 whole, which is shorter than its diff:
```python
import math

import jax
import jax.numpy as jnp
from jax import lax
from jax.experimental import pallas as pl
from jax.experimental.pallas import tpu as pltpu
from jax.sharding import PartitionSpec as P

MESH = pl.DeviceIdType.MESH
SBX, SBY, SBZ = 4, 4, 2
BLK = 128
NB = SBX * SBY * SBZ
EX, EY, EZ = SBX + 2, SBY + 2, SBZ + 2
NE = EX * EY * EZ
CELLS = 1024
AXES = ("gx", "gy", "gz")

inner_step = 0.1
gauss_width = 0.25
pair_scale = 0.1
soften = 1.0
coulomb = 0.02
half_step = 0.5 * inner_step
outer_half = 2.0 * inner_step

rate = 1.0 / (2.0 * gauss_width * gauss_width)
bits = rate / math.log(2.0)
pair_factor = pair_scale / (gauss_width * gauss_width) * math.exp(-rate) / (bits * bits)

FACES = ((-1, 0, 0), (1, 0, 0), (0, -1, 0), (0, 1, 0), (0, 0, -1), (0, 0, 1))
AROUND = tuple(
    (dx, dy, dz)
    for dx in (-1, 0, 1)
    for dy in (-1, 0, 1)
    for dz in (-1, 0, 1)
    if (dx, dy, dz) != (0, 0, 0)
)
SIZES = (4, 8, 4)

F32 = jnp.float32
BF16 = jnp.bfloat16


def row_ids(n=4):
    return lax.broadcasted_iota(jnp.int32, (n, BLK), 0)


def rows4(a, b, c, d):
    r = row_ids()
    return jnp.where(r == 0, a, jnp.where(r == 1, b, jnp.where(r == 2, c, d)))


def place(b):
    return b // (SBY * SBZ) + 1, b // SBZ % SBY + 1, b % SBZ + 1


def lane_gather(values, lanes):
    numbers = lax.GatherDimensionNumbers(
        offset_dims=(),
        collapsed_slice_dims=(1,),
        start_index_map=(1,),
        operand_batching_dims=(0,),
        start_indices_batching_dims=(0,),
    )
    return lax.gather(
        values,
        lanes[..., None],
        numbers,
        slice_sizes=(1, 1),
        mode=lax.GatherScatterMode.PROMISE_IN_BOUNDS,
    )


def thirds(value):
    high = value.astype(BF16).astype(F32)
    rest = value - high
    middle = rest.astype(BF16).astype(F32)
    return high, middle, rest - middle


def send_box(step, inner, ghost):
    count = inner
    if step == 0:
        return 1, count
    if ghost:
        return (0 if step > 0 else count + 1), 1
    return (count if step > 0 else 1), 1


def box(direction, ghost):
    return [send_box(s, inner, ghost) for s, inner in zip(direction, (SBX, SBY, SBZ))]


def cut(where, lines=4):
    return tuple(pl.ds(start, size) for start, size in where) + (pl.ds(0, lines), slice(None))


def spots(where):
    (x, nx), (y, ny), (z, nz) = where
    return [(x + i, y + j, z + k) for i in range(nx) for j in range(ny) for k in range(nz)]


def flat(x, y, z):
    return (x * EY + y) * EZ + z


ORDER = sorted(AROUND, key=lambda d: (d[1] != 0, d[2] != 0, d))
SENDS = ORDER[::-1]
ORDER_Y = next(i for i, d in enumerate(ORDER) if d[1] != 0)


def kernel(
    pos_h,
    vel_h,
    stren_h,
    chg_h,
    stiff_h,
    part_h,
    bforce_h,
    pforce_h,
    fforce_h,
    frac_h,
    pairs_h,
    cell_h,
    count_h,
    xo,
    vo,
    pos,
    vel,
    stren,
    chg,
    stiff,
    part,
    bforce,
    pforce,
    fforce,
    frac,
    frac_s,
    pairs,
    cell,
    count,
    hood0,
    hood1,
    hood2,
    hood3,
    vbuf,
    qbuf,
    slots,
    aways,
    springs,
    near,
    pull,
    left,
    centre,
    part0,
    part1,
    part2,
    got0,
    got1,
    got2,
    ins,
    hs,
    hr,
    gs,
    gr,
    ms,
    mr,
):
    me = tuple(lax.axis_index(a) for a in AXES)

    def device(shift):
        return tuple(lax.rem(m + (s + n), n) for m, s, n in zip(me, shift, SIZES))

    barrier = pltpu.get_barrier_semaphore()
    peers = set(AROUND)
    for axis, n in ((2, 4), (0, 4), (1, 8)):
        for o in range(2, n - 1):
            peers.add(tuple(o if a == axis else 0 for a in range(3)))
    peers = sorted(peers)
    for shift in peers:
        pl.semaphore_signal(barrier, inc=1, device_id=device(shift), device_id_type=MESH)

    fetches = [
        pltpu.make_async_copy(source, target, ins.at[i])
        for i, (source, target) in enumerate(
            (
                (count_h, count),
                (pos_h, pos),
                (vel_h, vel),
                (fforce_h, fforce),
                (pforce_h, pforce),
                (bforce_h, bforce),
                (stren_h, stren),
                (part_h, part),
                (stiff_h, stiff),
                (chg_h, chg),
                (pairs_h, pairs),
                (cell_h, cell),
                (frac_h, frac),
                (frac_h, frac_s),
            )
        )
    ]
    for copy in fetches:
        copy.start()

    rows = row_ids()
    xyz = rows < 3
    lanes = lax.broadcasted_iota(jnp.int32, (1, BLK), 1)
    rows8 = row_ids(8)
    upper = rows8 < 4

    def halo(hood, which, directions, lines):
        return {
            d: pltpu.make_async_remote_copy(
                src_ref=hood.at[cut(box(d, False), lines)],
                dst_ref=hood.at[cut(box(d, True), lines)],
                send_sem=hs.at[which, AROUND.index(d)],
                recv_sem=hr.at[which, AROUND.index(d)],
                device_id=device(d),
                device_id_type=MESH,
            )
            for d in directions
        }

    def launch(copies):
        for d in SENDS:
            if d in copies:
                copies[d].start()

    def shift_of(d):
        return rows4(-SBX * d[0] * 1.0, -SBY * d[1] * 1.0, -SBZ * d[2] * 1.0, 0.0)

    def begin(b, _):
        px, py, pz = place(b)
        live = jnp.where(b * BLK + lanes < count[0], 1.0, 0.0)
        x = rows4(pos[0, b], pos[1, b], pos[2, b], stren[b] * live)
        v = [
            vel[d, b]
            + outer_half * fforce[d, b]
            + inner_step * pforce[d, b]
            + half_step * bforce[d, b]
            for d in range(3)
        ]
        v = rows4(v[0], v[1], v[2], 0.0)
        vbuf[b] = v
        hood0[px, py, pz] = x + inner_step * v
        return 0

    for copy in fetches[:7]:
        copy.wait()
    lax.fori_loop(0, NB, begin, 0, unroll=4)
    pl.semaphore_wait(barrier, len(peers))
    copies0 = halo(hood0, 0, FACES, 3)
    launch(copies0)

    for copy in fetches[7:]:
        copy.wait()

    def bonds(b, _):
        px, py, pz = place(b)
        live = jnp.where(b * BLK + lanes < count[0], 1.0, 0.0)
        qbuf[b] = chg[b] * live
        columns = jnp.where(upper, part[0, b], part[1, b])
        slots[b] = columns & (BLK - 1)
        aways[b] = jnp.where((rows8 & 3) < 3, (columns >> 7) - flat(px, py, pz), NE)
        spring = jnp.where(upper, stiff[0, b], stiff[1, b])
        springs[b] = jnp.where((rows8 & 3) < 3, spring, 0.0)
        return 0

    lax.fori_loop(0, NB, bonds, 0, unroll=4)
    for d in range(3):
        for k in range(8):
            centre[d, k : k + 1, :] = frac[d : d + 1, k * BLK : (k + 1) * BLK] * (
                1.0 * SIZES[d] * (SBX, SBY, SBZ)[d]
            )

    def pick(tile, b, d):
        twice = jnp.concatenate([tile, tile], axis=0)
        offset = (d[0] * EY + d[1]) * EZ + d[2]
        return twice, aways[b] == offset, lane_gather(twice, slots[b])

    def fold(value):
        return value[0:4] + value[4:8]

    def bond_inside(hood, size):
        for b in range(NB):
            p = tuple(int(i) for i in place(b))
            own, hit, other = pick(hood[p], b, (0, 0, 0))
            other = jnp.where(hit, other, 0.0)
            for d in FACES:
                q = tuple(i + j for i, j in zip(p, d))
                if all(1 <= i <= n for i, n in zip(q, (SBX, SBY, SBZ))):
                    _, hit, value = pick(hood[q], b, d)
                    other = jnp.where(hit, value, other)
            vbuf[b] = vbuf[b] + size * fold(springs[b] * (other - own))

    def bond_face(hood, size, d):
        shift = shift_of(d)
        for q in spots(box(d, True)):
            e = tuple(-i for i in d)
            p = tuple(i + j for i, j in zip(q, d))
            b = ((p[0] - 1) * SBY + p[1] - 1) * SBZ + p[2] - 1
            _, hit, value = pick(hood[q] + shift, b, e)
            vbuf[b] = vbuf[b] + size * fold(jnp.where(hit, springs[b] * value, 0.0))

    def drift(hood, after):
        for b in range(NB):
            p = tuple(int(i) for i in place(b))
            after[p] = hood[p] + inner_step * vbuf[b]

    middle = rows4(0.5 * SBX, 0.5 * SBY, 0.5 * SBZ, 0.0)
    ones = jnp.where(xyz, 1.0, 0.0)
    blank = jnp.zeros((4, BLK), F32)

    def square_sum(z):
        return jnp.sum(jnp.where(xyz, z * z, 0.0), axis=0, keepdims=True)

    def prepare(e, z, a):
        high, mid, low = thirds(jnp.where(xyz, z, -bits * square_sum(z)))
        near[e] = jnp.concatenate(
            [high, mid, low, high, mid, high, ones, blank], axis=0
        ).astype(BF16)
        high, mid, low = thirds(jnp.where(xyz, z * a, a))
        pull[e] = jnp.concatenate([high, mid, low, blank], axis=0).astype(BF16)

    def prepare_ghosts(hood, d):
        shift = shift_of(d) - middle
        for q in spots(box(d, True)):
            prepare(flat(*q), hood[q] + shift, hood1[q][3:4])

    def prepare_own(hood):
        def body(b, _):
            px, py, pz = place(b)
            tile = hood[px, py, pz]
            z = tile - middle
            prepare(flat(px, py, pz), z, tile[3:4])
            high, mid, low = thirds(jnp.where(xyz, (2.0 * bits) * z, 1.0))
            ph, pm, pw = thirds(bits - bits * square_sum(z))
            stack = jnp.concatenate(
                [high, high, high, mid, mid, low, rows4(ph, pm, pw, 0.0), blank], axis=0
            )
            left[b] = stack.T.astype(BF16)
            return 0

        lax.fori_loop(0, NB, body, 0, unroll=4)

    def pair(hood, c, p):
        listed = [pairs[k, c] for k in range(8)]
        t = jnp.dot(
            left[c],
            jnp.concatenate([near[e] for e in listed], axis=1),
            preferred_element_type=F32,
        )
        r = jnp.maximum(t, 0.0)
        w = jnp.exp2(t) * (r * r)
        high = w.astype(BF16)
        low = (w - high.astype(F32)).astype(BF16)
        y = jnp.concatenate([pull[e] for e in listed], axis=1)
        over = (((1,), (1,)), ((), ()))
        acc = lax.dot_general(high, y, over, preferred_element_type=F32)
        acc = acc + lax.dot_general(low, y, over, preferred_element_type=F32)
        s = acc.T
        f = s[0:4] + s[4:8] + s[8:12]
        tile = hood[p]
        z = tile - middle
        force = (pair_factor * tile[3:4]) * (z * f[3:4] - f)
        return tile, jnp.where(xyz, force, 0.0)

    def pair_groups(hood, body):
        def group(g, _):
            by = jnp.where(g == 0, 0, jnp.where(g == 1, SBY - 1, g - 1))
            for bx in range(SBX):
                for bz in range(SBZ):
                    c = (bx * SBY + by) * SBZ + bz
                    p = (bx + 1, by + 1, bz + 1)
                    body(c, p, *pair(hood, c, p))
            return by

        return group

    bond_inside(hood0, inner_step)
    for d in ORDER:
        if d in copies0:
            copies0[d].wait_recv()
            bond_face(hood0, inner_step, d)
    drift(hood0, hood1)
    copies1 = halo(hood1, 1, AROUND, 4)
    launch(copies1)
    prepare_own(hood1)
    bond_inside(hood1, inner_step)
    for d in ORDER:
        copies1[d].wait_recv()
        prepare_ghosts(hood1, d)
        if d in FACES:
            bond_face(hood1, inner_step, d)

    def pieces(by, g):
        found = []
        for i, d in enumerate(FACES):
            if d[1] == 0:
                src, dst = box(d, False), box(d, True)
                src[1] = dst[1] = (by + 1, 1)
                found.append(
                    pltpu.make_async_remote_copy(
                        src_ref=hood2.at[cut(src, 3)],
                        dst_ref=hood2.at[cut(dst, 3)],
                        send_sem=gs.at[g, i],
                        recv_sem=gr.at[g, i],
                        device_id=device(d),
                        device_id_type=MESH,
                    )
                )
        return found

    copies2 = halo(hood2, 2, ((0, -1, 0), (0, 1, 0)), 3)

    def kick_drift(c, p, tile, force):
        v = vbuf[c] + (2.0 * inner_step) * force
        vbuf[c] = v
        hood2[p] = tile + inner_step * v

    first = pair_groups(hood1, kick_drift)

    def first_group(g, _):
        by = first(g, 0)

        @pl.when(g == 0)
        def _():
            copies2[(0, -1, 0)].start()

        @pl.when(g == 1)
        def _():
            copies2[(0, 1, 0)].start()

        for copy in pieces(by, g):
            copy.start()
        return 0

    lax.fori_loop(0, SBY, first_group, 0)
    parts2 = [pieces(by, g) for g, by in enumerate((0, SBY - 1, 1, 2))]
    bond_inside(hood2, inner_step)
    for i, d in enumerate([d for d in FACES if d[1] == 0]):
        for group in parts2:
            group[i].wait_recv()
        bond_face(hood2, inner_step, d)
    for d in copies2:
        copies2[d].wait_recv()
        bond_face(hood2, inner_step, d)
    drift(hood2, hood3)
    copies3 = halo(hood3, 3, AROUND, 3)
    launch(copies3)

    cell_ids = lax.broadcasted_iota(jnp.int32, (8, BLK), 0) * BLK + lax.broadcasted_iota(
        jnp.int32, (8, BLK), 1
    )
    corner = rows4(
        (me[0] * SBX).astype(F32), (me[1] * SBY).astype(F32), (me[2] * SBZ).astype(F32), 0.0
    )

    def gather_moments(b, totals):
        px, py, pz = place(b)
        tile = hood3[px, py, pz]
        for d in range(3):
            xo[d, b] = tile[d : d + 1]
        sums = jnp.sum(
            qbuf[b] * jnp.where(xyz, tile + corner, 1.0), axis=1, keepdims=True
        )
        here = cell_ids == cell[b]
        return tuple(
            total + jnp.where(here, sums[d : d + 1], 0.0) for d, total in enumerate(totals)
        )

    zero = jnp.zeros((8, BLK), F32)
    moments = lax.fori_loop(0, NB, gather_moments, (zero, zero, zero, zero), unroll=4)
    for d in range(4):
        part0[d] = moments[d]

    stages = ((2, 4, part0, got0, 0), (0, 4, part1, got1, 3), (1, 8, part2, got2, 6))

    def spread(stage):
        axis, n, mine, got, base = stages[stage]
        return [
            pltpu.make_async_remote_copy(
                src_ref=mine,
                dst_ref=got.at[o - 1],
                send_sem=ms.at[base + o - 1],
                recv_sem=mr.at[base + o - 1],
                device_id=device(tuple(o if a == axis else 0 for a in range(3))),
                device_id_type=MESH,
            )
            for o in range(1, n)
        ]

    spreads = [spread(stage) for stage in range(3)]

    def send_moments(stage):
        for copy in spreads[stage]:
            copy.start()

    def collect(stage):
        axis, n, mine, got, base = stages[stage]
        for copy in spreads[stage]:
            copy.wait_recv()
        total = mine[...]
        for o in range(1, n):
            total = total + got[o - 1]
        return total

    send_moments(0)
    prepare_own(hood3)
    bond_inside(hood3, half_step)

    for d in ORDER:
        if d == ORDER[ORDER_Y]:
            part1[...] = collect(0)
            send_moments(1)
        copies3[d].wait_recv()
        prepare_ghosts(hood3, d)
        if d in FACES:
            bond_face(hood3, half_step, d)

    def kick(c, p, tile, force):
        vbuf[c] = vbuf[c] + inner_step * force

    second = pair_groups(hood3, kick)

    def second_group(g, _):
        second(g, 0)

        @pl.when(g == 0)
        def _():
            part2[...] = collect(1)
            send_moments(2)

        return 0

    lax.fori_loop(0, SBY, second_group, 0)
    totals = collect(2)

    charge_sum = totals[3]
    places = [centre[d] for d in range(3)]
    dipole = [totals[d] - charge_sum * places[d] for d in range(3)]

    def finish(b, _):
        target = cell[b]
        away = [
            frac_s[d, target] * (1.0 * SIZES[d] * (SBX, SBY, SBZ)[d]) - places[d]
            for d in range(3)
        ]
        inverse = lax.rsqrt(
            away[0] * away[0] + away[1] * away[1] + away[2] * away[2] + soften * soften
        )
        cube = inverse * inverse * inverse
        fifth = cube * inverse * inverse
        along = dipole[0] * away[0] + dipole[1] * away[1] + dipole[2] * away[2]
        gain = charge_sum * cube + 3.0 * along * fifth
        field = [
            jnp.sum(gain * away[d] - dipole[d] * cube, axis=(0, 1), keepdims=True)
            for d in range(3)
        ]
        size = (outer_half * coulomb) * qbuf[b]
        v = vbuf[b]
        for d in range(3):
            vo[d, b] = v[d : d + 1] + size * field[d]
        return 0

    lax.fori_loop(0, NB, finish, 0, unroll=4)

    sent = [copies[d] for copies in (copies0, copies1, copies2, copies3) for d in copies]
    for copies in parts2 + spreads:
        sent += copies
    for copy in sent:
        copy.wait_send()


def per_device(
    positions,
    velocities,
    strength,
    charge,
    bond_stiffness,
    bond_partner,
    pair_blocks,
    tile_count,
    block_cell,
    cell_frac,
    bond_force,
    pair_force,
    far_force,
):
    lines = lambda value, n: value.reshape(n, NB, 1, BLK)
    vmem = pl.BlockSpec(memory_space=pltpu.VMEM)
    anywhere = pl.BlockSpec(memory_space=pl.ANY)
    hood = pltpu.VMEM((EX, EY, EZ, 4, BLK), F32)
    line3 = pltpu.VMEM((3, NB, 1, BLK), F32)
    line2 = pltpu.VMEM((2, NB, 1, BLK), F32)
    line1 = pltpu.VMEM((NB, 1, BLK), F32)
    sums = pltpu.VMEM((4, 8, BLK), F32)
    out = jax.ShapeDtypeStruct((3, NB, 1, BLK), F32)
    x, v = pl.pallas_call(
        kernel,
        out_shape=(out, out),
        in_specs=[anywhere] * 13,
        out_specs=(vmem, vmem),
        scratch_shapes=[
            line3,
            line3,
            line1,
            line1,
            line2,
            pltpu.VMEM((2, NB, 1, BLK), jnp.int32),
            line3,
            line3,
            line3,
            pltpu.VMEM((3, CELLS), F32),
            pltpu.SMEM((3, CELLS), F32),
            pltpu.SMEM((8, NB), jnp.int32),
            pltpu.SMEM((NB,), jnp.int32),
            pltpu.SMEM((1,), jnp.int32),
            hood,
            hood,
            hood,
            hood,
            pltpu.VMEM((NB, 4, BLK), F32),
            line1,
            pltpu.VMEM((NB, 8, BLK), jnp.int32),
            pltpu.VMEM((NB, 8, BLK), jnp.int32),
            pltpu.VMEM((NB, 8, BLK), F32),
            pltpu.VMEM((NE, 32, BLK), BF16),
            pltpu.VMEM((NE, 16, BLK), BF16),
            pltpu.VMEM((NB, BLK, 32), BF16),
            pltpu.VMEM((3, 8, BLK), F32),
            sums,
            sums,
            sums,
            pltpu.VMEM((3, 4, 8, BLK), F32),
            pltpu.VMEM((3, 4, 8, BLK), F32),
            pltpu.VMEM((7, 4, 8, BLK), F32),
            pltpu.SemaphoreType.DMA((14,)),
            pltpu.SemaphoreType.DMA((4, 26)),
            pltpu.SemaphoreType.DMA((4, 26)),
            pltpu.SemaphoreType.DMA((4, 6)),
            pltpu.SemaphoreType.DMA((4, 6)),
            pltpu.SemaphoreType.DMA((13,)),
            pltpu.SemaphoreType.DMA((13,)),
        ],
        compiler_params=pltpu.CompilerParams(
            collective_id=0, has_side_effects=True, vmem_limit_bytes=60 * 1024 * 1024
        ),
        name="outer_step",
    )(
        lines(positions, 3),
        lines(velocities, 3),
        strength.reshape(NB, 1, BLK),
        charge.reshape(NB, 1, BLK),
        lines(bond_stiffness, 2),
        lines(bond_partner, 2),
        lines(bond_force, 3),
        lines(pair_force, 3),
        lines(far_force, 3),
        cell_frac,
        pair_blocks.reshape(NB, 8).T,
        block_cell.reshape(NB),
        tile_count.reshape(1),
    )
    return x.reshape(positions.shape), v.reshape(velocities.shape)


def solution(mesh):
    vector = P(None, "gx", "gy", "gz", None)
    scalar = P("gx", "gy", "gz", None)
    in_specs = (
        vector,
        vector,
        scalar,
        scalar,
        vector,
        vector,
        P("gx", "gy", "gz", None, None),
        P("gx", "gy", "gz"),
        scalar,
        P(),
        vector,
        vector,
        vector,
    )
    return jax.shard_map(
        per_device, mesh=mesh, in_specs=in_specs, out_specs=(vector, vector), check_vma=False
    )
```

time: 82.9 us -> 55.6 us (0.67)
  Pallas kernels: 72 us -> 52 us
  local copies, waits for them, and re-layouts: 8.86 us -> 2.06 us
    pallas_call x1, Pallas kernels: 72 us -> 52 us  [per_device(): pl.pallas_call(kernel, out_shape=(out, out), in_specs=[anywhere] * 13, ou...]
    unnamed x27 -> x4, local copies, waits for them, and re-layouts: 8.86 us -> 2.06 us
where the time goes in v1:
time: 55.6 us; the launch traced here: 55.4 us
  Pallas kernels  52 us (94%)
  local copies, waits for them, and re-layouts  2.06 us (4%)
  between operations  1.3 us (2%)
    pallas_call x1, Pallas kernels, per_device(): pl.pallas_call(kernel, out_shape=(out, out), in_specs=[anywhere] * 13, ou...  52 us
    unnamed x4, local copies, waits for them, and re-layouts  2.06 us

profile of v1, /device:TPU:1, one launch (start us, length us, event | category | flops | bytes accessed | tf_op | source)
XLA Modules:
  0.0 55.4 jit_solution(1594659737344362425)
XLA Ops:
  1.3 52.0 %outer_step.1 = (f32[3,32,1,128]{3,2,1,0:T(1,128)}, f32[3,32,1,128]{3,2,1,0:T(1,128)}) custom-call(f32[3,32,1,128]{3,2,1,0:T(1,128)} %bitcast.23, f32[3,32,1,128]{3,2,1,0:T(1,128)} %bitcast.24, f32[32,1,128]{2,1,0:T(1,128)} %bitcast.30, f32[32,1,128]{2,1,0:T(1,128)} %bitcast.31, f32[2,32,1,128]{3,2,1,0:T(1,128)} %bitcast.28, s32[2,32,1,128]{3,2,1,0:T(1,128)} %bitcast.29, ...), custom_call_target="tpu_custom_call" | custom-call | tf_op jit(solution)/shard_map/outer_step/pallas_call | solution.py:602
  53.3 0.0 copy-start
  53.3 1.4 %copy.22 = f32[3,1,1,1,4096]{4,3,2,1,0:T(1,128)} copy(f32[3,1,1,1,4096]{4,3,2,1,0:T(1,128)} %bitcast.22) | data formatting | bytes 98304
  54.8 0.0 copy-done
  54.8 0.6 %copy.23 = f32[3,1,1,1,4096]{4,3,2,1,0:T(1,128)} copy(f32[3,1,1,1,4096]{4,3,2,1,0:T(1,128)S(1)} %bitcast.21) | data formatting | bytes 98304
Async XLA Ops:
  53.3 1.4 %copy-start = (f32[3,32,1,128]{3,2,1,0:T(1,128)S(1)}, f32[3,32,1,128]{3,2,1,0:T(1,128)}, u32[]{:S(2)}) copy-start(f32[3,32,1,128]{3,2,1,0:T(1,128)} %get-tuple-element.5) | copy-start | bytes 147460

commit v2 on v1

--- a/solution.py
+++ b/solution.py
@@ -92,6 +92,13 @@
     return [send_box(s, inner, ghost) for s, inner in zip(direction, (SBX, SBY, SBZ))]
 
 
+def part_box(direction, ghost, rows):
+    where = box(direction, ghost)
+    if direction[1] == 0:
+        where[1] = (rows[0] + 1, rows[1])
+    return where
+
+
 def cut(where, lines=4):
     return tuple(pl.ds(start, size) for start, size in where) + (pl.ds(0, lines), slice(None))
 
@@ -124,8 +131,7 @@
     pairs_h,
     cell_h,
     count_h,
-    xo,
-    vo,
+    oo,
     pos,
     vel,
     stren,
@@ -164,6 +170,8 @@
     hr,
     gs,
     gr,
+    rs,
+    rr,
     ms,
     mr,
 ):
@@ -296,19 +304,20 @@
                     other = jnp.where(hit, value, other)
             vbuf[b] = vbuf[b] + size * fold(springs[b] * (other - own))
 
-    def bond_face(hood, size, d):
+    def bond_face(hood, size, d, rows=(0, SBY)):
         shift = shift_of(d)
-        for q in spots(box(d, True)):
+        for q in spots(part_box(d, True, rows)):
             e = tuple(-i for i in d)
             p = tuple(i + j for i, j in zip(q, d))
             b = ((p[0] - 1) * SBY + p[1] - 1) * SBZ + p[2] - 1
             _, hit, value = pick(hood[q] + shift, b, e)
             vbuf[b] = vbuf[b] + size * fold(jnp.where(hit, springs[b] * value, 0.0))
 
-    def drift(hood, after):
+    def drift(hood, after, row=None):
         for b in range(NB):
             p = tuple(int(i) for i in place(b))
-            after[p] = hood[p] + inner_step * vbuf[b]
+            if row is None or p[1] == row + 1:
+                after[p] = hood[p] + inner_step * vbuf[b]
 
     middle = rows4(0.5 * SBX, 0.5 * SBY, 0.5 * SBZ, 0.0)
     ones = jnp.where(xyz, 1.0, 0.0)
@@ -325,9 +334,9 @@
         high, mid, low = thirds(jnp.where(xyz, z * a, a))
         pull[e] = jnp.concatenate([high, mid, low, blank], axis=0).astype(BF16)
 
-    def prepare_ghosts(hood, d):
+    def prepare_ghosts(hood, d, rows=(0, SBY)):
         shift = shift_of(d) - middle
-        for q in spots(box(d, True)):
+        for q in spots(part_box(d, True, rows)):
             prepare(flat(*q), hood[q] + shift, hood1[q][3:4])
 
     def prepare_own(hood):
@@ -368,17 +377,12 @@
         force = (pair_factor * tile[3:4]) * (z * f[3:4] - f)
         return tile, jnp.where(xyz, force, 0.0)
 
-    def pair_groups(hood, body):
-        def group(g, _):
-            by = jnp.where(g == 0, 0, jnp.where(g == 1, SBY - 1, g - 1))
-            for bx in range(SBX):
-                for bz in range(SBZ):
-                    c = (bx * SBY + by) * SBZ + bz
-                    p = (bx + 1, by + 1, bz + 1)
-                    body(c, p, *pair(hood, c, p))
-            return by
-
-        return group
+    def pair_row(hood, by, body):
+        for bx in range(SBX):
+            for bz in range(SBZ):
+                c = (bx * SBY + by) * SBZ + bz
+                p = (bx + 1, by + 1, bz + 1)
+                body(c, p, *pair(hood, c, p))
 
     bond_inside(hood0, inner_step)
     for d in ORDER:
@@ -390,68 +394,76 @@
     launch(copies1)
     prepare_own(hood1)
     bond_inside(hood1, inner_step)
-    for d in ORDER:
+    def take1(d):
         copies1[d].wait_recv()
         prepare_ghosts(hood1, d)
         if d in FACES:
             bond_face(hood1, inner_step, d)
 
-    def pieces(by, g):
-        found = []
-        for i, d in enumerate(FACES):
-            if d[1] == 0:
-                src, dst = box(d, False), box(d, True)
-                src[1] = dst[1] = (by + 1, 1)
-                found.append(
-                    pltpu.make_async_remote_copy(
-                        src_ref=hood2.at[cut(src, 3)],
-                        dst_ref=hood2.at[cut(dst, 3)],
-                        send_sem=gs.at[g, i],
-                        recv_sem=gr.at[g, i],
-                        device_id=device(d),
-                        device_id_type=MESH,
-                    )
-                )
-        return found
-
+    def row_copies(hood, directions, by, sends, recvs):
+        rows = (by, 1)
+        return {
+            d: pltpu.make_async_remote_copy(
+                src_ref=hood.at[cut(part_box(d, False, rows), 3)],
+                dst_ref=hood.at[cut(part_box(d, True, rows), 3)],
+                send_sem=sends.at[by, i],
+                recv_sem=recvs.at[by, i],
+                device_id=device(d),
+                device_id_type=MESH,
+            )
+            for i, d in enumerate(directions)
+        }
+
+    flat_faces = [d for d in FACES if d[1] == 0]
     copies2 = halo(hood2, 2, ((0, -1, 0), (0, 1, 0)), 3)
+    parts2 = [row_copies(hood2, flat_faces, by, gs, gr) for by in range(SBY)]
 
     def kick_drift(c, p, tile, force):
         v = vbuf[c] + (2.0 * inner_step) * force
         vbuf[c] = v
         hood2[p] = tile + inner_step * v
 
-    first = pair_groups(hood1, kick_drift)
-
-    def first_group(g, _):
-        by = first(g, 0)
+    for d in ORDER[:ORDER_Y]:
+        take1(d)
+
+    def first_row(g, _):
+        by = jnp.where(g == 0, 1, jnp.where(g == 1, 0, jnp.where(g == 2, SBY - 1, 2)))
+        pair_row(hood1, by, kick_drift)
 
         @pl.when(g == 0)
         def _():
-            copies2[(0, -1, 0)].start()
+            for d in ORDER[ORDER_Y:]:
+                take1(d)
 
         @pl.when(g == 1)
         def _():
+            copies2[(0, -1, 0)].start()
+
+        @pl.when(g == 2)
+        def _():
             copies2[(0, 1, 0)].start()
 
-        for copy in pieces(by, g):
+        for copy in row_copies(hood2, flat_faces, by, gs, gr).values():
             copy.start()
         return 0
 
-    lax.fori_loop(0, SBY, first_group, 0)
-    parts2 = [pieces(by, g) for g, by in enumerate((0, SBY - 1, 1, 2))]
+    lax.fori_loop(0, SBY, first_row, 0)
+    copies3 = halo(hood3, 3, [d for d in AROUND if d[1] != 0], 3)
+    flat_around = [d for d in AROUND if d[1] == 0]
+    parts3 = [row_copies(hood3, flat_around, by, rs, rr) for by in range(SBY)]
     bond_inside(hood2, inner_step)
-    for i, d in enumerate([d for d in FACES if d[1] == 0]):
-        for group in parts2:
-            group[i].wait_recv()
-        bond_face(hood2, inner_step, d)
-    for d in copies2:
-        copies2[d].wait_recv()
-        bond_face(hood2, inner_step, d)
-    drift(hood2, hood3)
-    copies3 = halo(hood3, 3, AROUND, 3)
-    launch(copies3)
-
+    for by in (1, SBY - 1, 0, 2):
+        for d in flat_faces:
+            parts2[by][d].wait_recv()
+            bond_face(hood2, inner_step, d, (by, 1))
+        if by in (0, SBY - 1):
+            d = (0, 1, 0) if by == 0 else (0, -1, 0)
+            copies2[d].wait_recv()
+            bond_face(hood2, inner_step, d)
+        drift(hood2, hood3, by)
+        if by in (0, SBY - 1):
+            launch({d: copies3[d] for d in copies3 if d[1] == (-1 if by == 0 else 1)})
+        launch(parts3[by])
     cell_ids = lax.broadcasted_iota(jnp.int32, (8, BLK), 0) * BLK + lax.broadcasted_iota(
         jnp.int32, (8, BLK), 1
     )
@@ -463,7 +475,7 @@
         px, py, pz = place(b)
         tile = hood3[px, py, pz]
         for d in range(3):
-            xo[d, b] = tile[d : d + 1]
+            oo[d, b] = tile[d : d + 1]
         sums = jnp.sum(
             qbuf[b] * jnp.where(xyz, tile + corner, 1.0), axis=1, keepdims=True
         )
@@ -512,31 +524,43 @@
     prepare_own(hood3)
     bond_inside(hood3, half_step)
 
-    for d in ORDER:
-        if d == ORDER[ORDER_Y]:
+    def take3(copies, d, rows=(0, SBY)):
+        copies[d].wait_recv()
+        prepare_ghosts(hood3, d, rows)
+        if d in FACES:
+            bond_face(hood3, half_step, d, rows)
+
+    def kick(c, p, tile, force):
+        vbuf[c] = vbuf[c] + inner_step * force
+
+    for by in (1, SBY - 1, 0):
+        for d in flat_around:
+            take3(parts3[by], d, (by, 1))
+    for d in ORDER[ORDER_Y:]:
+        if d[1] > 0:
+            take3(copies3, d)
+
+    def second_row(by, _):
+        pair_row(hood3, by, kick)
+
+        @pl.when(by == 0)
+        def _():
             part1[...] = collect(0)
             send_moments(1)
-        copies3[d].wait_recv()
-        prepare_ghosts(hood3, d)
-        if d in FACES:
-            bond_face(hood3, half_step, d)
-
-    def kick(c, p, tile, force):
-        vbuf[c] = vbuf[c] + inner_step * force
-
-    second = pair_groups(hood3, kick)
-
-    def second_group(g, _):
-        second(g, 0)
-
-        @pl.when(g == 0)
+            for d in flat_around:
+                take3(parts3[2], d, (2, 1))
+            for d in ORDER[ORDER_Y:]:
+                if d[1] < 0:
+                    take3(copies3, d)
+
+        @pl.when(by == 1)
         def _():
             part2[...] = collect(1)
             send_moments(2)
 
         return 0
 
-    lax.fori_loop(0, SBY, second_group, 0)
+    lax.fori_loop(0, SBY, second_row, 0)
     totals = collect(2)
 
     charge_sum = totals[3]
@@ -563,13 +587,15 @@
         size = (outer_half * coulomb) * qbuf[b]
         v = vbuf[b]
         for d in range(3):
-            vo[d, b] = v[d : d + 1] + size * field[d]
+            oo[3 + d, b] = v[d : d + 1] + size * field[d]
         return 0
 
     lax.fori_loop(0, NB, finish, 0, unroll=4)
 
     sent = [copies[d] for copies in (copies0, copies1, copies2, copies3) for d in copies]
-    for copies in parts2 + spreads:
+    for copies in parts2 + parts3:
+        sent += copies.values()
+    for copies in spreads:
         sent += copies
     for copy in sent:
         copy.wait_send()
@@ -599,11 +625,11 @@
     line1 = pltpu.VMEM((NB, 1, BLK), F32)
     sums = pltpu.VMEM((4, 8, BLK), F32)
     out = jax.ShapeDtypeStruct((3, NB, 1, BLK), F32)
-    x, v = pl.pallas_call(
+    xv = pl.pallas_call(
         kernel,
-        out_shape=(out, out),
+        out_shape=jax.ShapeDtypeStruct((6, NB, 1, BLK), F32),
         in_specs=[anywhere] * 13,
-        out_specs=(vmem, vmem),
+        out_specs=vmem,
         scratch_shapes=[
             line3,
             line3,
@@ -641,8 +667,10 @@
             pltpu.SemaphoreType.DMA((14,)),
             pltpu.SemaphoreType.DMA((4, 26)),
             pltpu.SemaphoreType.DMA((4, 26)),
-            pltpu.SemaphoreType.DMA((4, 6)),
-            pltpu.SemaphoreType.DMA((4, 6)),
+            pltpu.SemaphoreType.DMA((4, 4)),
+            pltpu.SemaphoreType.DMA((4, 4)),
+            pltpu.SemaphoreType.DMA((4, 8)),
+            pltpu.SemaphoreType.DMA((4, 8)),
             pltpu.SemaphoreType.DMA((13,)),
             pltpu.SemaphoreType.DMA((13,)),
         ],
@@ -665,7 +693,7 @@
         block_cell.reshape(NB),
         tile_count.reshape(1),
     )
-    return x.reshape(positions.shape), v.reshape(velocities.shape)
+    return xv[:3].reshape(positions.shape), xv[3:].reshape(velocities.shape)
 
 
 def solution(mesh):

time: 55.6 us -> 54 us (0.971)
  Pallas kernels: 52 us -> 51 us
  local copies, waits for them, and re-layouts: 2.06 us -> 1.47 us
    pallas_call x1, Pallas kernels: 52 us -> 51 us  [per_device(): pl.pallas_call(kernel, out_shape=jax.ShapeDtypeStruct((6, NB, 1, BLK), F3...]
    unnamed x4 -> x1, local copies, waits for them, and re-layouts: 2.06 us -> 1.47 us
where the time goes in v2:
time: 54 us; the launch traced here: 53.8 us
  Pallas kernels  51 us (94%)
  local copies, waits for them, and re-layouts  1.47 us (3%)
  between operations  1.29 us (2%)
    pallas_call x1, Pallas kernels, per_device(): pl.pallas_call(kernel, out_shape=jax.ShapeDtypeStruct((6, NB, 1, BLK), F3...  51 us
    unnamed x1, local copies, waits for them, and re-layouts  1.47 us

profile of v2, /device:TPU:1, one launch (start us, length us, event | category | flops | bytes accessed | tf_op | source)
XLA Modules:
  0.0 53.8 jit_solution(7475260058341504537)
XLA Ops:
  1.3 51.0 %outer_step.1 = f32[6,32,1,128]{3,2,1,0:T(1,128)} custom-call(f32[3,32,1,128]{3,2,1,0:T(1,128)} %bitcast.23, f32[3,32,1,128]{3,2,1,0:T(1,128)} %bitcast.24, f32[32,1,128]{2,1,0:T(1,128)} %bitcast.30, f32[32,1,128]{2,1,0:T(1,128)} %bitcast.31, f32[2,32,1,128]{3,2,1,0:T(1,128)} %bitcast.28, s32[2,32,1,128]{3,2,1,0:T(1,128)} %bitcast.29, ...), custom_call_target="tpu_custom_call" | custom-call | tf_op jit(solution)/shard_map/outer_step/pallas_call | solution.py:628
  52.3 1.5 %slice_bitcast_fusion = (f32[3,1,1,1,4096]{4,3,2,1,0:T(1,128)}, f32[3,1,1,1,4096]{4,3,2,1,0:T(1,128)}) fusion(f32[6,32,1,128]{3,2,1,0:T(1,128)} %outer_step.1), kind=kLoop, calls=%fused_computation | loop fusion | bytes 196608

commit v3 on v2

--- a/solution.py
+++ b/solution.py
@@ -353,7 +353,7 @@
             left[b] = stack.T.astype(BF16)
             return 0
 
-        lax.fori_loop(0, NB, body, 0, unroll=4)
+        lax.fori_loop(0, NB, body, 0, unroll=8)
 
     def pair(hood, c, p):
         listed = [pairs[k, c] for k in range(8)]
@@ -368,8 +368,10 @@
         low = (w - high.astype(F32)).astype(BF16)
         y = jnp.concatenate([pull[e] for e in listed], axis=1)
         over = (((1,), (1,)), ((), ()))
-        acc = lax.dot_general(high, y, over, preferred_element_type=F32)
-        acc = acc + lax.dot_general(low, y, over, preferred_element_type=F32)
+        both = lax.dot_general(
+            jnp.concatenate([high, low], axis=0), y, over, preferred_element_type=F32
+        )
+        acc = both[0:BLK] + both[BLK : 2 * BLK]
         s = acc.T
         f = s[0:4] + s[4:8] + s[8:12]
         tile = hood[p]
@@ -485,7 +487,7 @@
         )
 
     zero = jnp.zeros((8, BLK), F32)
-    moments = lax.fori_loop(0, NB, gather_moments, (zero, zero, zero, zero), unroll=4)
+    moments = lax.fori_loop(0, NB, gather_moments, (zero, zero, zero, zero), unroll=16)
     for d in range(4):
         part0[d] = moments[d]
 
@@ -590,7 +592,7 @@
             oo[3 + d, b] = v[d : d + 1] + size * field[d]
         return 0
 
-    lax.fori_loop(0, NB, finish, 0, unroll=4)
+    lax.fori_loop(0, NB, finish, 0, unroll=32)
 
     sent = [copies[d] for copies in (copies0, copies1, copies2, copies3) for d in copies]
     for copies in parts2 + parts3:

time: 54 us -> 51.1 us (0.946)
  Pallas kernels: 51 us -> 48.1 us
    pallas_call x1, Pallas kernels: 51 us -> 48.1 us  [per_device(): pl.pallas_call(kernel, out_shape=jax.ShapeDtypeStruct((6, NB, 1, BLK), F3...]
where the time goes in v3:
time: 51.1 us; the launch traced here: 50.8 us
  Pallas kernels  48.1 us (94%)
  local copies, waits for them, and re-layouts  1.47 us (3%)
  between operations  1.29 us (3%)
    pallas_call x1, Pallas kernels, per_device(): pl.pallas_call(kernel, out_shape=jax.ShapeDtypeStruct((6, NB, 1, BLK), F3...  48.1 us
    unnamed x1, local copies, waits for them, and re-layouts  1.47 us

profile of v3, /device:TPU:1, one launch (start us, length us, event | category | flops | bytes accessed | tf_op | source)
XLA Modules:
  0.0 50.8 jit_solution(12969261907031761832)
XLA Ops:
  1.3 48.1 %outer_step.1 = f32[6,32,1,128]{3,2,1,0:T(1,128)} custom-call(f32[3,32,1,128]{3,2,1,0:T(1,128)} %bitcast.23, f32[3,32,1,128]{3,2,1,0:T(1,128)} %bitcast.24, f32[32,1,128]{2,1,0:T(1,128)} %bitcast.30, f32[32,1,128]{2,1,0:T(1,128)} %bitcast.31, f32[2,32,1,128]{3,2,1,0:T(1,128)} %bitcast.28, s32[2,32,1,128]{3,2,1,0:T(1,128)} %bitcast.29, ...), custom_call_target="tpu_custom_call" | custom-call | tf_op jit(solution)/shard_map/outer_step/pallas_call | solution.py:630
  49.4 1.5 %slice_bitcast_fusion = (f32[3,1,1,1,4096]{4,3,2,1,0:T(1,128)}, f32[3,1,1,1,4096]{4,3,2,1,0:T(1,128)}) fusion(f32[6,32,1,128]{3,2,1,0:T(1,128)} %outer_step.1), kind=kLoop, calls=%fused_computation | loop fusion | bytes 196608

commit v4 on v3

--- a/solution.py
+++ b/solution.py
@@ -237,6 +237,11 @@
             if d in copies:
                 copies[d].start()
 
+    def drained(groups):
+        for group in groups:
+            for copy in group.values() if isinstance(group, dict) else group:
+                copy.wait_send()
+
     def shift_of(d):
         return rows4(-SBX * d[0] * 1.0, -SBY * d[1] * 1.0, -SBZ * d[2] * 1.0, 0.0)
 
@@ -394,6 +399,7 @@
     drift(hood0, hood1)
     copies1 = halo(hood1, 1, AROUND, 4)
     launch(copies1)
+    drained([copies0])
     prepare_own(hood1)
     bond_inside(hood1, inner_step)
     def take1(d):
@@ -523,8 +529,9 @@
         return total
 
     send_moments(0)
+    bond_inside(hood3, half_step)
     prepare_own(hood3)
-    bond_inside(hood3, half_step)
+    drained([copies1, copies2] + parts2)
 
     def take3(copies, d, rows=(0, SBY)):
         copies[d].wait_recv()
@@ -538,6 +545,8 @@
     for by in (1, SBY - 1, 0):
         for d in flat_around:
             take3(parts3[by], d, (by, 1))
+    part1[...] = collect(0)
+    send_moments(1)
     for d in ORDER[ORDER_Y:]:
         if d[1] > 0:
             take3(copies3, d)
@@ -547,15 +556,13 @@
 
         @pl.when(by == 0)
         def _():
-            part1[...] = collect(0)
-            send_moments(1)
             for d in flat_around:
                 take3(parts3[2], d, (2, 1))
             for d in ORDER[ORDER_Y:]:
                 if d[1] < 0:
                     take3(copies3, d)
 
-        @pl.when(by == 1)
+        @pl.when(by == 0)
         def _():
             part2[...] = collect(1)
             send_moments(2)
@@ -563,6 +570,7 @@
         return 0
 
     lax.fori_loop(0, SBY, second_row, 0)
+    drained([copies3] + parts3 + spreads[:2])
     totals = collect(2)
 
     charge_sum = totals[3]
@@ -594,13 +602,7 @@
 
     lax.fori_loop(0, NB, finish, 0, unroll=32)
 
-    sent = [copies[d] for copies in (copies0, copies1, copies2, copies3) for d in copies]
-    for copies in parts2 + parts3:
-        sent += copies.values()
-    for copies in spreads:
-        sent += copies
-    for copy in sent:
-        copy.wait_send()
+    drained(spreads[2:])
 
 
 def per_device(

time: 51.1 us -> 50.9 us (level)
  no operation moved by 1% of the time
where the time goes in v4:
time: 50.9 us; the launch traced here: 50.6 us
  Pallas kernels  47.9 us (94%)
  local copies, waits for them, and re-layouts  1.47 us (3%)
  between operations  1.29 us (3%)
    pallas_call x1, Pallas kernels, per_device(): pl.pallas_call(kernel, out_shape=jax.ShapeDtypeStruct((6, NB, 1, BLK), F3...  47.9 us
    unnamed x1, local copies, waits for them, and re-layouts  1.47 us

profile of v4, /device:TPU:1, one launch (start us, length us, event | category | flops | bytes accessed | tf_op | source)
XLA Modules:
  0.0 50.6 jit_solution(11060489508733259568)
XLA Ops:
  1.3 47.9 %outer_step.1 = f32[6,32,1,128]{3,2,1,0:T(1,128)} custom-call(f32[3,32,1,128]{3,2,1,0:T(1,128)} %bitcast.23, f32[3,32,1,128]{3,2,1,0:T(1,128)} %bitcast.24, f32[32,1,128]{2,1,0:T(1,128)} %bitcast.30, f32[32,1,128]{2,1,0:T(1,128)} %bitcast.31, f32[2,32,1,128]{3,2,1,0:T(1,128)} %bitcast.28, s32[2,32,1,128]{3,2,1,0:T(1,128)} %bitcast.29, ...), custom_call_target="tpu_custom_call" | custom-call | tf_op jit(solution)/shard_map/outer_step/pallas_call | solution.py:632
  49.2 1.5 %slice_bitcast_fusion = (f32[3,1,1,1,4096]{4,3,2,1,0:T(1,128)}, f32[3,1,1,1,4096]{4,3,2,1,0:T(1,128)}) fusion(f32[6,32,1,128]{3,2,1,0:T(1,128)} %outer_step.1), kind=kLoop, calls=%fused_computation | loop fusion | bytes 196608
